TPU v7x, 32 devices: a whole 2x2x4 slice. The times are simulated.
32 devices in a mesh: section: 4 (over y, core), dp: 8 (over z, x).
Axes of the slice: x: 2, y: 2, z: 4, core: 2. Of those that a mesh axis runs over, the one named last changes fastest.
Arguments:
- inputs: bfloat16 [1536, 4096], P('dp'), may hold values from -6 to 6
- output_cotangent: bfloat16 [1536, 4096], P('dp'), may hold values from -6 to 6
- lengths: int32 [16], P('dp'), may hold values from 24 to 96
- query_examples: int32 [16], replicated, may hold values from 0 to 15
- norm_gain: bfloat16 [4, 4096], P('section'), may hold values from 0.5 to 1.5
- value_weight: bfloat16 [4, 4096, 1024], P('section', 'dp'), may hold values from -0.09375 to 0.09375
- output_weight: bfloat16 [4, 4096, 1024], P('section', 'dp'), may hold values from -0.1875 to 0.1875
- input_projection: bfloat16 [4, 32, 4096], P('section'), may hold values from -0.09375 to 0.09375
- output_projection: bfloat16 [4, 32, 1024], P('section'), may hold values from -0.1875 to 0.1875
- fisher_prior: float32 [4, 1024, 1024], P('section'), as said below
Outputs:
- scores: float32 [16, 16], P('dp')
Inputs may be any that keep to these rules, and one draw needn't show every extreme that they name: `fisher_prior`: each block's 1024 x 1024 matrix is symmetric and positive definite.
All inputs are finite; a program needn't handle non-finite values.
Results may differ from a plain program's by a relative error of at most 0.0013.
Values may be sent and summed in bfloat16 or wider, within the bound.
A program may use at most 128 MiB of HBM per device.

v0:
```python
import jax
import jax.numpy as jnp
from jax import lax
from jax.sharding import PartitionSpec as P


def shifted(value, axis, steps):
    count = lax.axis_size(axis)
    first, last = (max(0, -steps), min(count, count - steps))
    return lax.ppermute(value, axis, [(source, source + steps) for source in range(first, last)])


def normalize(hidden, gain):
    widened = hidden.astype(jnp.float32)
    factor = lax.rsqrt(jnp.mean(widened * widened, axis=-1, keepdims=True) + 1e-05)
    return (widened * factor * gain.astype(jnp.float32)).astype(jnp.bfloat16)


def forward_block(hidden, gain, value_map, output_map, input_map):
    normed = normalize(hidden, gain)
    values = jnp.dot(normed, value_map, preferred_element_type=jnp.float32)
    activated = jax.nn.silu(values).astype(jnp.bfloat16)
    branch = lax.dot_general(
        activated, output_map, (((1,), (1,)), ((), ())), preferred_element_type=jnp.float32
    )
    following = (hidden.astype(jnp.float32) + branch).astype(jnp.bfloat16)
    features = lax.dot_general(
        normed, input_map, (((1,), (1,)), ((), ())), preferred_element_type=jnp.float32
    ).astype(jnp.bfloat16)
    return (following, values, features)


def backward_block(hidden, values, cotangent, gain, value_map, output_map, output_map_small):
    widened = hidden.astype(jnp.float32)
    factor = lax.rsqrt(jnp.mean(widened * widened, axis=-1, keepdims=True) + 1e-05)
    upstream = jnp.dot(cotangent, output_map, preferred_element_type=jnp.float32)
    logistic = jax.nn.sigmoid(values)
    slopes = (upstream * logistic * (1.0 + values * (1.0 - logistic))).astype(jnp.bfloat16)
    signals = lax.dot_general(
        slopes, output_map_small, (((1,), (1,)), ((), ())), preferred_element_type=jnp.float32
    ).astype(jnp.bfloat16)
    normed_grad = lax.dot_general(
        slopes, value_map, (((1,), (1,)), ((), ())), preferred_element_type=jnp.float32
    )
    weighted = normed_grad * gain.astype(jnp.float32)
    inner_mean = jnp.mean(weighted * widened, axis=-1, keepdims=True)
    hidden_grad = factor * weighted - widened * (factor * factor * factor) * inner_mean
    previous = (cotangent.astype(jnp.float32) + hidden_grad).astype(jnp.bfloat16)
    return (previous, signals)


def per_device(
    inputs,
    output_cotangent,
    lengths,
    query_examples,
    norm_gain,
    value_weight,
    output_weight,
    input_projection,
    output_projection,
    fisher_prior,
):
    sections = lax.axis_size("section")
    section_index = lax.axis_index("section")
    value_map, output_map = (
        lax.all_gather(value_weight, "dp", axis=1, tiled=True),
        lax.all_gather(output_weight, "dp", axis=1, tiled=True),
    )
    value_map = value_map[0]
    output_map = output_map[0]
    gain = norm_gain[0]
    input_map = input_projection[0]
    output_map_small = output_projection[0]
    prior_matrix = fisher_prior[0]
    batches = lengths.shape[0]
    example_rows = inputs.shape[0] // batches
    width = inputs.shape[1]
    value_width = value_map.shape[1]
    feature_width = input_map.shape[0]
    signal_width = output_map_small.shape[0]
    entries = inputs.reshape(batches, example_rows, width)
    positions = jnp.arange(example_rows, dtype=jnp.int32)
    keep = (positions[None, :] < lengths[:, None]).astype(jnp.bfloat16)
    targets = output_cotangent.reshape(batches, example_rows, width) * keep[:, :, None]
    ticks = batches + sections - 1

    def forward_running(hidden):
        return forward_block(hidden, gain, value_map, output_map, input_map)

    def forward_skipped(hidden):
        return (
            jnp.zeros_like(hidden),
            jnp.zeros((example_rows, value_width), jnp.float32),
            jnp.zeros((example_rows, feature_width), jnp.bfloat16),
        )

    def forward_tick(tick, carry):
        incoming, saved_hidden, saved_values, saved_features = carry
        turn = tick - section_index
        active = (turn >= 0) & (turn < batches)
        picked = jnp.clip(turn, 0, batches - 1)
        entering = lax.dynamic_index_in_dim(entries, picked, 0, keepdims=False)
        hidden = jnp.where(section_index == 0, entering, incoming)
        following, values, features = lax.cond(active, forward_running, forward_skipped, hidden)
        saved_hidden = jnp.where(
            active, lax.dynamic_update_index_in_dim(saved_hidden, hidden, picked, 0), saved_hidden
        )
        saved_values = jnp.where(
            active, lax.dynamic_update_index_in_dim(saved_values, values, picked, 0), saved_values
        )
        saved_features = jnp.where(
            active,
            lax.dynamic_update_index_in_dim(saved_features, features, picked, 0),
            saved_features,
        )
        incoming = shifted(following, "section", 1)
        return (incoming, saved_hidden, saved_values, saved_features)

    forward_start = (
        jnp.zeros((example_rows, width), jnp.bfloat16),
        jnp.zeros((batches, example_rows, width), jnp.bfloat16),
        jnp.zeros((batches, example_rows, value_width), jnp.float32),
        jnp.zeros((batches, example_rows, feature_width), jnp.bfloat16),
    )
    forward_state = lax.fori_loop(0, ticks, forward_tick, forward_start)
    saved_hidden = forward_state[1]
    saved_values = forward_state[2]
    saved_features = forward_state[3]

    def backward_running(operands):
        hidden, values, cotangent, features = operands
        previous, signals = backward_block(
            hidden, values, cotangent, gain, value_map, output_map, output_map_small
        )
        grads = (
            lax.dot_general(
                signals, features, (((0,), (0,)), ((), ())), preferred_element_type=jnp.float32
            )
            / example_rows
        )
        return (previous, grads)

    def backward_skipped(operands):
        return (
            jnp.zeros((example_rows, width), jnp.bfloat16),
            jnp.zeros((signal_width, feature_width), jnp.float32),
        )

    def backward_tick(tick, carry):
        incoming, saved_grads = carry
        turn = tick - (sections - 1 - section_index)
        active = (turn >= 0) & (turn < batches)
        picked = jnp.clip(turn, 0, batches - 1)
        arriving = lax.dynamic_index_in_dim(targets, picked, 0, keepdims=False)
        cotangent = jnp.where(section_index == sections - 1, arriving, incoming)
        hidden = lax.dynamic_index_in_dim(saved_hidden, picked, 0, keepdims=False)
        values = lax.dynamic_index_in_dim(saved_values, picked, 0, keepdims=False)
        features = lax.dynamic_index_in_dim(saved_features, picked, 0, keepdims=False)
        previous, grads = lax.cond(
            active, backward_running, backward_skipped, (hidden, values, cotangent, features)
        )
        saved_grads = jnp.where(
            active, lax.dynamic_update_index_in_dim(saved_grads, grads, picked, 0), saved_grads
        )
        incoming = shifted(previous, "section", -1)
        return (incoming, saved_grads)

    backward_start = (
        jnp.zeros((example_rows, width), jnp.bfloat16),
        jnp.zeros((batches, signal_width, feature_width), jnp.float32),
    )
    backward_state = lax.fori_loop(0, ticks, backward_tick, backward_start)
    flat = backward_state[1].reshape(batches, signal_width * feature_width)
    everyone = lax.all_gather(flat, "dp", axis=0, tiled=True)
    fisher = jnp.dot(everyone.T, everyone, precision=lax.Precision.HIGHEST)
    owners = jnp.arange(everyone.shape[0], dtype=jnp.int32)
    selector = (query_examples[:, None] == owners[None, :]).astype(jnp.float32)
    chosen = jnp.dot(selector, everyone, precision=lax.Precision.HIGHEST)
    hessian = prior_matrix + fisher
    lower_factor = jnp.linalg.cholesky(hessian)
    solved = jax.scipy.linalg.cho_solve((lower_factor, True), chosen.T)
    section_scores = jnp.dot(flat, solved, precision=lax.Precision.HIGHEST)
    return lax.psum(section_scores, "section")


def solution(mesh):
    placed = (
        P("dp", None),
        P("dp", None),
        P("dp"),
        P(),
        P("section", None),
        P("section", "dp", None),
        P("section", "dp", None),
        P("section", None, None),
        P("section", None, None),
        P("section", None, None),
    )
    return jax.shard_map(
        per_device, mesh=mesh, in_specs=placed, out_specs=P("dp", None), check_vma=False
    )
```

profile of v0, /device:TPU:0, one launch (start us, length us, event | category | flops | bytes accessed | tf_op | source)
XLA Modules:
  0.0 869.4 jit_solution(10538443919233326450)
XLA Ops:
  15.0 121.7 %all-gather.4.cloned.1.call-done = bf16[1,4096,1024]{2,1,0:T(8,128)(2,1)} async-done(((bf16[1,512,1024]{2,1,0:T(8,128)(2,1)}), bf16[1,4096,1024]{2,1,0:T(8,128)(2,1)}) %all-gather.4.cloned.1.call-update) | async-done | bytes 8388624 | tf_op jit(solution)/shard_map/all_gather | solution.py:67
  136.7 124.8 %all-gather.6.cloned.1.call-done = bf16[1,4096,1024]{2,1,0:T(8,128)(2,1)} async-done(((bf16[1,512,1024]{2,1,0:T(8,128)(2,1)}), bf16[1,4096,1024]{2,1,0:T(8,128)(2,1)}) %all-gather.6.cloned.1.call-update) | async-done | bytes 8388624 | tf_op jit(solution)/shard_map/all_gather | solution.py:68
  261.8 100.7 %while.38 = (s32[]{:T(128)}, bf16[96,4096]{1,0:T(8,128)(2,1)S(1)}, bf16[2,96,4096]{2,1,0:T(8,128)(2,1)S(1)}, f32[2,96,1024]{2,1,0:T(8,128)S(1)}, bf16[2,96,32]{1...) while((s32[]{:T(128)}, bf16[96,4096]{1,0:T(8,128)(2,1)S(1)}, ...), condition=%wide.region_4.5_spmd, body=%wide.region_0.4_spmd.sunk | while | flops 1642670208 | bytes 59466024 | solution.py:126
  298.7 18.6 %collective-permute-start = (bf16[96,4096]{1,0:T(8,128)(2,1)}, bf16[96,4096]{1,0:T(8,128)(2,1)S(1)}, u32[]{:S(2)}, u32[]{:S(2)}) collective-permute-start(bf16[96,4096]{1,0:T(8,128)(2,1)} %copy-done.2), channel_id=1, source_target_pairs={{0,8},{8,16},{16,24},{1,9},{9,17},{17,25},{2,10},{10,18},{18,26},{... | collective-permute-start | bytes 2359304 | tf_op jit(solution)/shard_map/while/body/eval_jaxpr/ppermute | solution.py:10
  322.7 11.4 %collective-permute-start = (bf16[96,4096]{1,0:T(8,128)(2,1)}, bf16[96,4096]{1,0:T(8,128)(2,1)S(1)}, u32[]{:S(2)}, u32[]{:S(2)}) collective-permute-start(bf16[96,4096]{1,0:T(8,128)(2,1)} %copy-done.2), channel_id=1, source_target_pairs={{0,8},{8,16},{16,24},{1,9},{9,17},{17,25},{2,10},{10,18},{18,26},{... | collective-permute-start | bytes 2359304 | tf_op jit(solution)/shard_map/while/body/eval_jaxpr/ppermute | solution.py:10
  339.5 20.9 %collective-permute-start = (bf16[96,4096]{1,0:T(8,128)(2,1)}, bf16[96,4096]{1,0:T(8,128)(2,1)S(1)}, u32[]{:S(2)}, u32[]{:S(2)}) collective-permute-start(bf16[96,4096]{1,0:T(8,128)(2,1)} %copy-done.2), channel_id=1, source_target_pairs={{0,8},{8,16},{16,24},{1,9},{9,17},{17,25},{2,10},{10,18},{18,26},{... | collective-permute-start | bytes 2359304 | tf_op jit(solution)/shard_map/while/body/eval_jaxpr/ppermute | solution.py:10
  362.7 100.6 %while.39 = (s32[]{:T(128)}, bf16[96,4096]{1,0:T(8,128)(2,1)S(1)}, f32[2,32,32]{2,1,0:T(8,128)S(1)}, s32[]{:T(128)}, pred[]{:T(512)}, /*index=5*/bf16[2,96,4096]...) while((s32[]{:T(128)}, bf16[96,4096]{1,0:T(8,128)(2,1)S(1)}, ...), condition=%wide.region_10.11_spmd, body=%wide.region_5.10_spmd.sunk | while | flops 1624286464 | bytes 69592752 | solution.py:173
  365.0 12.1 %collective-permute-done.1 = bf16[96,4096]{1,0:T(8,128)(2,1)S(1)} collective-permute-done((bf16[96,4096]{1,0:T(8,128)(2,1)}, bf16[96,4096]{1,0:T(8,128)(2,1)S(1)}, u32[]{:S(2)}, u32[]{:S(2)}) %collective-permute-start.1) | collective-permute-done | bytes 786464 | tf_op jit(solution)/shard_map/while/body/eval_jaxpr/ppermute | solution.py:10
  379.4 12.8 %collective-permute-done.1 = bf16[96,4096]{1,0:T(8,128)(2,1)S(1)} collective-permute-done((bf16[96,4096]{1,0:T(8,128)(2,1)}, bf16[96,4096]{1,0:T(8,128)(2,1)S(1)}, u32[]{:S(2)}, u32[]{:S(2)}) %collective-permute-start.1) | collective-permute-done | bytes 786464 | tf_op jit(solution)/shard_map/while/body/eval_jaxpr/ppermute | solution.py:10
  394.5 29.7 %collective-permute-done.1 = bf16[96,4096]{1,0:T(8,128)(2,1)S(1)} collective-permute-done((bf16[96,4096]{1,0:T(8,128)(2,1)}, bf16[96,4096]{1,0:T(8,128)(2,1)S(1)}, u32[]{:S(2)}, u32[]{:S(2)}) %collective-permute-start.1) | collective-permute-done | bytes 786464 | tf_op jit(solution)/shard_map/while/body/eval_jaxpr/ppermute | solution.py:10
  424.2 10.6 %conditional.5 = (bf16[96,4096]{1,0:T(8,128)(2,1)}, f32[1,32,32]{2,1,0:T(8,128)S(1)}) conditional(s32[]{:T(128)} %convert_element_type.113, () %tuple.153, (pred[]{:T(512)}, bf16[2,96,4096]{2,1,0:T(8,128)(2,1)}, s32[]{:T(128)}, bf16[96,4096]{1,0:T(8,128)(2,1)S(1)}, bf16[2,96,4096]{2,1,0:T(8,128)(2,1)S(1)}, /*index=5*/bf16[4096,1024]{1,0:T(8,128)(2,1)}, ...), branch_computations={%region_6.6_spmd, %region_7.9_spmd} | conditional | flops 1624285440 | bytes 66397524 | solution.py:160
  436.2 12.2 %collective-permute-done.1 = bf16[96,4096]{1,0:T(8,128)(2,1)S(1)} collective-permute-done((bf16[96,4096]{1,0:T(8,128)(2,1)}, bf16[96,4096]{1,0:T(8,128)(2,1)S(1)}, u32[]{:S(2)}, u32[]{:S(2)}) %collective-permute-start.1) | collective-permute-done | bytes 786464 | tf_op jit(solution)/shard_map/while/body/eval_jaxpr/ppermute | solution.py:10
  463.5 30.5 %all-gather = f32[8,2,1024]{2,1,0:T(2,128)S(1)} all-gather(f32[1,2,1024]{2,1,0:T(2,128)S(1)} %reshape.190), channel_id=1, replica_groups=mesh['section'=4,'dp'=8] {'dp'}, dimensions={0}, use_global_device_ids=true | all-gather | bytes 73728 | tf_op jit(solution)/shard_map/all_gather | solution.py:175
  512.5 11.7 %cholesky.223 = f32[128,128]{1,0:T(8,128)S(1)} custom-call(f32[128,128]{1,0:T(8,128)S(1)} %cholesky.580), custom_call_target="Cholesky" | custom-call | tf_op jit(solution)/shard_map/jit(cholesky)/cholesky | solution.py:181
  540.6 11.9 %cholesky.244 = f32[128,128]{1,0:T(8,128)S(1)} custom-call(f32[128,128]{1,0:T(8,128)S(1)} %cholesky.584), custom_call_target="Cholesky" | custom-call | tf_op jit(solution)/shard_map/jit(cholesky)/cholesky | solution.py:181
  566.3 11.7 %cholesky.468 = f32[128,128]{1,0:T(8,128)S(1)} custom-call(f32[128,128]{1,0:T(8,128)S(1)} %cholesky.589), custom_call_target="Cholesky" | custom-call | tf_op jit(solution)/shard_map/jit(cholesky)/cholesky | solution.py:181
  592.6 12.1 %cholesky.487 = f32[128,128]{1,0:T(8,128)S(1)} custom-call(f32[128,128]{1,0:T(8,128)S(1)} %cholesky.594), custom_call_target="Cholesky" | custom-call | tf_op jit(solution)/shard_map/jit(cholesky)/cholesky | solution.py:181
  619.3 11.7 %cholesky.506 = f32[128,128]{1,0:T(8,128)S(1)} custom-call(f32[128,128]{1,0:T(8,128)S(1)} %cholesky.599), custom_call_target="Cholesky" | custom-call | tf_op jit(solution)/shard_map/jit(cholesky)/cholesky | solution.py:181
  645.5 11.7 %cholesky.526 = f32[128,128]{1,0:T(8,128)S(1)} custom-call(f32[128,128]{1,0:T(8,128)S(1)} %cholesky.604), custom_call_target="Cholesky" | custom-call | tf_op jit(solution)/shard_map/jit(cholesky)/cholesky | solution.py:181
  671.3 11.9 %cholesky.546 = f32[128,128]{1,0:T(8,128)S(1)} custom-call(f32[128,128]{1,0:T(8,128)S(1)} %cholesky.609), custom_call_target="Cholesky" | custom-call | tf_op jit(solution)/shard_map/jit(cholesky)/cholesky | solution.py:181
  696.9 11.7 %cholesky.564 = f32[128,128]{1,0:T(8,128)S(1)} custom-call(f32[128,128]{1,0:T(8,128)S(1)} %convolution_subtract_fusion.6), custom_call_target="Cholesky" | custom-call | tf_op jit(solution)/shard_map/jit(cholesky)/cholesky | solution.py:181
  720.3 27.6 %while.40 = (s32[]{:T(128)}, f32[1024,1024]{1,0:T(8,128)}, s32[8,2]{0,1:T(2,128)S(1)}, f32[8,128,128]{2,1,0:T(8,128)}, s32[]{:T(128)}) while((s32[]{:T(128)}, f32[1024,1024]{1,0:T(8,128)}, s32[8,2]{0,1:T(2,128)S(1)}, f32[8,128,128]{2,1,0:T(8,128)}, s32[]{:T(128)}) %tuple.167), condition=%wide.while_cond, body=%wide.while_body.sunk | while | flops 2 | bytes 132705 | solution.py:182
  747.9 79.6 %custom-call.73 = f32[8,128,128]{1,2,0:T(8,128)S(1)} custom-call(f32[8,128,128]{2,1,0:T(8,128)} %get-tuple-element.657), custom_call_target="InvertDiagBlocksLowerTriangular" | custom-call | tf_op jit(solution)/shard_map/jit(_cho_solve)/triangular_solve | solution.py:182
  849.1 13.0 %psum.7 = f32[2,16]{1,0:T(2,128)} all-reduce(f32[2,16]{1,0:T(2,128)S(1)} %fusion.127), channel_id=1, replica_groups=mesh['section'=4,'dp'=8] {'section'}, use_global_device_ids=true, to_apply=%region_27.28 | all-reduce | flops 32 | bytes 256 | tf_op jit(solution)/shard_map/psum | solution.py:184
  (272 shorter events, 304.6 us)
Async XLA Ops:
  6.5 130.2 %all-gather.4.cloned.1.call-start = ((), (), s32[]{:S(2)}) async-start(), calls=%async_computation | async-start | bytes 9437184 | tf_op jit(solution)/shard_map/all_gather | solution.py:67
  7.3 254.2 %all-gather.6.cloned.1.call-start = ((), (), s32[]{:S(2)}) async-start(), calls=%async_computation.1 | async-start | bytes 9437184 | tf_op jit(solution)/shard_map/all_gather | solution.py:68
  8.0 5.5 copy-start.6
  8.0 5.6 copy-start.9
  8.0 5.6 copy-start.5
  261.8 100.9 %copy-start.4 = (bf16[1,32,1024]{2,1,0:T(8,128)(2,1)S(1)}, bf16[1,32,1024]{2,1,0:T(8,128)(2,1)}, u32[]{:S(2)}) copy-start(bf16[1,32,1024]{2,1,0:T(8,128)(2,1)} %param.26) | copy-start | bytes 196612
  263.5 6.1 slice-start
  263.8 5.8 slice-start.1
  274.7 3.4 collective-permute-start
  279.7 6.1 slice-start
  280.0 5.8 slice-start.1
  285.8 3.8 copy-start.8
  291.0 4.4 collective-permute-start
  298.7 20.6 %collective-permute-start = (bf16[96,4096]{1,0:T(8,128)(2,1)}, bf16[96,4096]{1,0:T(8,128)(2,1)S(1)}, u32[]{:S(2)}, u32[]{:S(2)}) collective-permute-start(bf16[96,4096]{1,0:T(8,128)(2,1)} %copy-done.2), channel_id=1, source_target_pairs={{0,8},{8,16},{16,24},{1,9},{9,17},{17,25},{2,10},{10,18},{18,26},{... | collective-permute-start | bytes 2359304 | tf_op jit(solution)/shard_map/while/body/eval_jaxpr/ppermute | solution.py:10
  322.7 13.5 %collective-permute-start = (bf16[96,4096]{1,0:T(8,128)(2,1)}, bf16[96,4096]{1,0:T(8,128)(2,1)S(1)}, u32[]{:S(2)}, u32[]{:S(2)}) collective-permute-start(bf16[96,4096]{1,0:T(8,128)(2,1)} %copy-done.2), channel_id=1, source_target_pairs={{0,8},{8,16},{16,24},{1,9},{9,17},{17,25},{2,10},{10,18},{18,26},{... | collective-permute-start | bytes 2359304 | tf_op jit(solution)/shard_map/while/body/eval_jaxpr/ppermute | solution.py:10
  339.5 23.0 %collective-permute-start = (bf16[96,4096]{1,0:T(8,128)(2,1)}, bf16[96,4096]{1,0:T(8,128)(2,1)S(1)}, u32[]{:S(2)}, u32[]{:S(2)}) collective-permute-start(bf16[96,4096]{1,0:T(8,128)(2,1)} %copy-done.2), channel_id=1, source_target_pairs={{0,8},{8,16},{16,24},{1,9},{9,17},{17,25},{2,10},{10,18},{18,26},{... | collective-permute-start | bytes 2359304 | tf_op jit(solution)/shard_map/while/body/eval_jaxpr/ppermute | solution.py:10
  363.7 13.4 %collective-permute-start.1 = (bf16[96,4096]{1,0:T(8,128)(2,1)}, bf16[96,4096]{1,0:T(8,128)(2,1)S(1)}, u32[]{:S(2)}, u32[]{:S(2)}) collective-permute-start(bf16[96,4096]{1,0:T(8,128)(2,1)} %get-tuple-element.996), channel_id=1, source_target_pairs={{8,0},{16,8},{24,16},{9,1},{17,9},{25,17},{10,2},{18,10},{26,18},{... | collective-permute-start | bytes 2359304 | tf_op jit(solution)/shard_map/while/body/eval_jaxpr/ppermute | solution.py:10
  378.1 14.1 %collective-permute-start.1 = (bf16[96,4096]{1,0:T(8,128)(2,1)}, bf16[96,4096]{1,0:T(8,128)(2,1)S(1)}, u32[]{:S(2)}, u32[]{:S(2)}) collective-permute-start(bf16[96,4096]{1,0:T(8,128)(2,1)} %get-tuple-element.996), channel_id=1, source_target_pairs={{8,0},{16,8},{24,16},{9,1},{17,9},{25,17},{10,2},{18,10},{26,18},{... | collective-permute-start | bytes 2359304 | tf_op jit(solution)/shard_map/while/body/eval_jaxpr/ppermute | solution.py:10
  393.2 31.1 %collective-permute-start.1 = (bf16[96,4096]{1,0:T(8,128)(2,1)}, bf16[96,4096]{1,0:T(8,128)(2,1)S(1)}, u32[]{:S(2)}, u32[]{:S(2)}) collective-permute-start(bf16[96,4096]{1,0:T(8,128)(2,1)} %get-tuple-element.996), channel_id=1, source_target_pairs={{8,0},{16,8},{24,16},{9,1},{17,9},{25,17},{10,2},{18,10},{26,18},{... | collective-permute-start | bytes 2359304 | tf_op jit(solution)/shard_map/while/body/eval_jaxpr/ppermute | solution.py:10
  424.2 6.0 copy-start
  434.8 13.5 %collective-permute-start.1 = (bf16[96,4096]{1,0:T(8,128)(2,1)}, bf16[96,4096]{1,0:T(8,128)(2,1)S(1)}, u32[]{:S(2)}, u32[]{:S(2)}) collective-permute-start(bf16[96,4096]{1,0:T(8,128)(2,1)} %get-tuple-element.996), channel_id=1, source_target_pairs={{8,0},{16,8},{24,16},{9,1},{17,9},{25,17},{10,2},{18,10},{26,18},{... | collective-permute-start | bytes 2359304 | tf_op jit(solution)/shard_map/while/body/eval_jaxpr/ppermute | solution.py:10
  448.4 6.0 copy-start
  459.0 4.4 collective-permute-start.1
  715.5 112.1 %copy-start.7 = (s32[16]{0:T(128)S(1)}, s32[16]{0:T(128)}, u32[]{:S(2)}) copy-start(s32[16]{0:T(128)} %param.21) | copy-start | bytes 196
  (9 other events, 15.8 us)
Sparse Core Ops, SparseCore 0:
  9.5 127.1 all-gather.3
  138.8 122.6 all-gather.5
where the time goes:
time: 880 us; the launch traced here: 869 us
  waiting for transfers between devices  326 us (37%)
  other arithmetic  277 us (31%)
  matrix products  87.4 us (10%)
  starting transfers between devices  61.1 us (7%)
  local copies, waits for them, and re-layouts  55.5 us (6%)
  blocking collectives  43.6 us (5%)
  between operations  19.2 us (2%)
    another operation x30, other arithmetic, per_device(): lower_factor = jnp.linalg.cholesky(hessian)  172 us
    all_gather x1, waiting for transfers between devices, per_device(): lax.all_gather(output_weight, 'dp', axis=1, tiled=True)  125 us
    all_gather x1, waiting for transfers between devices, per_device(): lax.all_gather(value_weight, 'dp', axis=1, tiled=True)  122 us
    another operation x3, other arithmetic, per_device(): solved = jax.scipy.linalg.cho_solve((lower_factor, True), chosen.T)  84.4 us
    ppermute x10, waiting for transfers between devices, shifted(): lax.ppermute(value, axis, [(source, source + steps) for source in range(f...  77.7 us
    ppermute x10, starting transfers between devices, shifted(): lax.ppermute(value, axis, [(source, source + steps) for source in range(f...  61 us
    another operation x32, local copies, waits for them, and re-layouts  30.8 us
    all_gather x1, blocking collectives, per_device(): everyone = lax.all_gather(flat, 'dp', axis=0, tiled=True)  30.5 us
  transfers between devices with their start and end apart: 12, of which 12 were waited for; matrix products, arithmetic and copies ran while one was open for 1% of the time, Pallas kernels for 0%

commit v1 on v0

--- a/solution.py
+++ b/solution.py
@@ -1,7 +1,112 @@
 import jax
 import jax.numpy as jnp
 from jax import lax
+from jax.experimental import pallas as pl
+from jax.experimental.pallas import tpu as pltpu
 from jax.sharding import PartitionSpec as P
+
+
+HIGHEST = lax.Precision.HIGHEST
+
+
+def inverted(block):
+    size = block.shape[0]
+    rows = lax.broadcasted_iota(jnp.int32, block.shape, 0)
+    columns = lax.broadcasted_iota(jnp.int32, block.shape, 1)
+
+    def sweep(pivot, held):
+        at_row, at_column = rows == pivot, columns == pivot
+        row = jnp.sum(jnp.where(at_row, held, 0.0), axis=0, keepdims=True)
+        column = jnp.sum(jnp.where(at_column, held, 0.0), axis=1, keepdims=True)
+        corner = jnp.sum(jnp.where(at_column[:1], row, 0.0), axis=1, keepdims=True)
+        scale = 1.0 / corner
+        scaled = row * scale
+        updated = held - column * scaled
+        updated = jnp.where(at_row, scaled, updated)
+        updated = jnp.where(at_column, column * scale, updated)
+        return jnp.where(at_row & at_column, -scale, updated)
+
+    return -lax.fori_loop(0, size, sweep, block)
+
+
+def invert_in_place(work, strip, block):
+    size = work.shape[0]
+    count = size // block
+
+    def eliminate(step, carry):
+        span = pl.ds(pl.multiple_of(step * block, block), block)
+        corner = inverted(work[span, span])
+        strip[...] = jnp.dot(
+            corner, work[span, :], precision=HIGHEST, preferred_element_type=jnp.float32
+        )
+
+        def update(other, carry):
+            across = pl.ds(pl.multiple_of(other * block, block), block)
+            lead = work[span, across].T
+
+            @pl.when(other != step)
+            def _():
+                work[across, :] -= jnp.dot(
+                    lead, strip[...], precision=HIGHEST, preferred_element_type=jnp.float32
+                )
+                work[across, span] = strip[:, across].T
+
+            return carry
+
+        lax.fori_loop(0, count, update, 0)
+        work[span, :] = strip[...]
+        work[span, span] = -corner
+        return carry
+
+    lax.fori_loop(0, count, eliminate, 0)
+
+
+def prior_kernel(prior, work, strip):
+    work[...] = prior[...]
+    invert_in_place(work, strip, strip.shape[0])
+
+
+def prior_inverse(prior):
+    size = prior.shape[0]
+    block = 128
+    return pl.pallas_call(
+        prior_kernel,
+        out_shape=jax.ShapeDtypeStruct((size, size), jnp.float32),
+        in_specs=[pl.BlockSpec(memory_space=pltpu.VMEM)],
+        out_specs=pl.BlockSpec(memory_space=pltpu.VMEM),
+        scratch_shapes=[pltpu.VMEM((block, size), jnp.float32)],
+        compiler_params=pltpu.CompilerParams(vmem_limit_bytes=24 * 2**20),
+        cost_estimate=pl.CostEstimate(flops=10**11, bytes_accessed=8 * size * size, transcendentals=0),
+        name="prior_inverse",
+    )(prior)
+
+
+def score_kernel(everyone, negated, queries, out):
+    grads = everyone[...]
+    half = jnp.dot(grads, negated[...], precision=HIGHEST, preferred_element_type=jnp.float32)
+    gram = -lax.dot_general(
+        half, grads, (((1,), (1,)), ((), ())), precision=HIGHEST,
+        preferred_element_type=jnp.float32,
+    )
+    count = grads.shape[0]
+    rows = lax.broadcasted_iota(jnp.int32, (count, count), 0)
+    columns = lax.broadcasted_iota(jnp.int32, (count, count), 1)
+    inverse = inverted(gram + jnp.where(rows == columns, 1.0, 0.0))
+    full = jnp.dot(gram, inverse, precision=HIGHEST, preferred_element_type=jnp.float32)
+    owners = lax.broadcasted_iota(jnp.int32, (count, queries.shape[1]), 0)
+    selector = jnp.where(owners == queries[...], 1.0, 0.0)
+    out[...] = jnp.dot(full, selector, precision=HIGHEST, preferred_element_type=jnp.float32)
+
+
+def all_scores(everyone, negated, queries):
+    return pl.pallas_call(
+        score_kernel,
+        out_shape=jax.ShapeDtypeStruct((everyone.shape[0], queries.shape[0]), jnp.float32),
+        in_specs=[pl.BlockSpec(memory_space=pltpu.VMEM)] * 3,
+        out_specs=pl.BlockSpec(memory_space=pltpu.VMEM),
+        compiler_params=pltpu.CompilerParams(vmem_limit_bytes=24 * 2**20),
+        name="all_scores",
+    )(everyone, negated, queries[None, :])
 
 
 def shifted(value, axis, steps):
@@ -72,7 +177,7 @@
     gain = norm_gain[0]
     input_map = input_projection[0]
     output_map_small = output_projection[0]
-    prior_matrix = fisher_prior[0]
+    negated_inverse = prior_inverse(fisher_prior[0])
     batches = lengths.shape[0]
     example_rows = inputs.shape[0] // batches
     width = inputs.shape[1]
@@ -173,14 +278,10 @@
     backward_state = lax.fori_loop(0, ticks, backward_tick, backward_start)
     flat = backward_state[1].reshape(batches, signal_width * feature_width)
     everyone = lax.all_gather(flat, "dp", axis=0, tiled=True)
-    fisher = jnp.dot(everyone.T, everyone, precision=lax.Precision.HIGHEST)
-    owners = jnp.arange(everyone.shape[0], dtype=jnp.int32)
-    selector = (query_examples[:, None] == owners[None, :]).astype(jnp.float32)
-    chosen = jnp.dot(selector, everyone, precision=lax.Precision.HIGHEST)
-    hessian = prior_matrix + fisher
-    lower_factor = jnp.linalg.cholesky(hessian)
-    solved = jax.scipy.linalg.cho_solve((lower_factor, True), chosen.T)
-    section_scores = jnp.dot(flat, solved, precision=lax.Precision.HIGHEST)
+    every_score = all_scores(everyone, negated_inverse, query_examples)
+    section_scores = lax.dynamic_slice_in_dim(
+        every_score, lax.axis_index("dp") * batches, batches, 0
+    )
     return lax.psum(section_scores, "section")
 
 

time: 880 us -> 522 us (0.59); the launches traced: 869 us -> 521 us
  other arithmetic: 277 us -> 15.7 us
  Pallas kernels: 0 us -> 176 us
  waiting for transfers between devices: 326 us -> 156 us
  matrix products: 87.4 us -> 38.5 us
  local copies, waits for them, and re-layouts: 55.5 us -> 17 us
    another operation x33 -> x0, other arithmetic: 257 us -> none  [the longest x30 172 us: per_device(): lower_factor = jnp.linalg.cholesky(hessian)]
    pallas_call x0 -> x2, Pallas kernels: none -> 176 us  [the longest x1 172 us: prior_inverse(): pl.pallas_call(prior_kernel, out_shape=jax.ShapeDtypeStruct((size, size),...]
    all_gather x1, waiting for transfers between devices: 122 us -> 0.01 us  [per_device(): lax.all_gather(value_weight, 'dp', axis=1, tiled=True)]
    all_gather x1, waiting for transfers between devices: 125 us -> 76.3 us  [per_device(): lax.all_gather(output_weight, 'dp', axis=1, tiled=True)]
    another operation x44 -> x0, matrix products: 43.8 us -> none  [the longest x14 23.1 us: per_device(): lower_factor = jnp.linalg.cholesky(hessian)]
    another operation x45 -> x8, local copies, waits for them, and re-layouts: 33.4 us -> 6.04 us
  transfers between devices with their start and end apart: 12 -> 12, of which waited for: 12 -> 11; matrix products, arithmetic and copies ran while one was open for 1% -> 1% of each run, Pallas kernels for 0% -> 33%
where the time goes in v1:
time: 522 us; the launch traced here: 521 us
  Pallas kernels  176 us (34%)
  waiting for transfers between devices  156 us (30%)
  starting transfers between devices  61 us (12%)
  blocking collectives  43.4 us (8%)
  matrix products  38.5 us (7%)
  local copies, waits for them, and re-layouts  17 us (3%)
  other arithmetic  15.7 us (3%)
  between operations  13.5 us (3%)
    pallas_call x1, Pallas kernels, prior_inverse(): pl.pallas_call(prior_kernel, out_shape=jax.ShapeDtypeStruct((size, size),...  172 us
    ppermute x10, waiting for transfers between devices, shifted(): lax.ppermute(value, axis, [(source, source + steps) for source in range(f...  77.9 us
    all_gather x1, waiting for transfers between devices, per_device(): lax.all_gather(output_weight, 'dp', axis=1, tiled=True)  76.3 us
    ppermute x10, starting transfers between devices, shifted(): lax.ppermute(value, axis, [(source, source + steps) for source in range(f...  61 us
    all_gather x1, blocking collectives, per_device(): everyone = lax.all_gather(flat, 'dp', axis=0, tiled=True)  30.5 us
    psum x1, blocking collectives, per_device(): return lax.psum(section_scores, 'section')  12.9 us
    dot_general x2, matrix products, forward_block(): values = jnp.dot(normed, value_map, preferred_element_type=jnp.float32)  11.6 us
  transfers between devices with their start and end apart: 12, of which 11 were waited for; matrix products, arithmetic and copies ran while one was open for 1% of the time, Pallas kernels for 33%

profile of v1, /device:TPU:0, one launch (start us, length us, event | category | flops | bytes accessed | tf_op | source)
XLA Modules:
  0.0 520.9 jit_solution(5402564499315407977)
XLA Ops:
  11.7 171.7 %prior_inverse.1.negated = f32[1024,1024]{1,0:T(8,128)S(1)} custom-call(f32[1024,1024]{1,0:T(8,128)S(1)} %bitcast.59), custom_call_target="tpu_custom_call" | custom-call | flops 99999997952 | bytes 8388608 | tf_op jit(solution)/shard_map/prior_inverse/pallas_call | solution.py:72
  185.3 76.3 %all-gather.6.cloned.1.call-done = bf16[1,4096,1024]{2,1,0:T(8,128)(2,1)} async-done(((bf16[1,512,1024]{2,1,0:T(8,128)(2,1)}), bf16[1,4096,1024]{2,1,0:T(8,128)(2,1)}) %all-gather.6.cloned.1.call-update) | async-done | bytes 8388624 | tf_op jit(solution)/shard_map/all_gather | solution.py:173
  262.0 100.9 %while.37 = (s32[]{:T(128)}, bf16[96,4096]{1,0:T(8,128)(2,1)S(1)}, bf16[2,96,4096]{2,1,0:T(8,128)(2,1)S(1)}, f32[2,96,1024]{2,1,0:T(8,128)S(1)}, bf16[2,96,32]{1...) while((s32[]{:T(128)}, bf16[96,4096]{1,0:T(8,128)(2,1)S(1)}, ...), condition=%wide.region_4.5_spmd, body=%wide.region_0.4_spmd.sunk | while | flops 1642670208 | bytes 56320268 | solution.py:231
  263.7 11.2 %conditional.4 = (bf16[96,4096]{1,0:T(8,128)(2,1)}, f32[1,96,1024]{2,1,0:T(8,128)}, bf16[1,96,32]{1,2,0:T(8,128)(2,1)S(1)}) conditional(s32[]{:T(128)} %convert_element_type.111, () %tuple.101, (bf16[96,4096]{1,0:T(8,128)(2,1)S(1)}, bf16[4096]{0:T(1024)(128)(2,1)S(1)}, bf16[4096,1024]{1,0:T(8,128)(2,1)}, bf16[4096,1024]{1,0:T(8,128)(2,1)}, ...), branch_computations={%region_1.1_spmd, %region_2.3_spmd} | conditional | flops 1641782400 | bytes 46989256 | solution.py:210
  264.0 5.8 %fusion.6 = f32[96,1024]{1,0:T(8,128)} fusion(bf16[4096,1024]{1,0:T(8,128)(2,1)} %get-tuple-element.596, bf16[96,4096]{1,0:T(8,128)(2,1)S(1)} %get-tuple-element.594, f32[4096]{0:T(1024)S(1)} %convert_element_type.61, f32[96]{0:T(128)S(1)} %add_rsqrt_fusion), kind=kOutput, calls=%fused_computation.10 | convolution fusion | flops 806879232 | bytes 9585024 | tf_op jit(solution)/shard_map/while/body/eval_jaxpr/cond/branch_1_fun/dot_general | solution.py:126
  269.8 4.6 fusion
  280.0 11.2 %conditional.4 = (bf16[96,4096]{1,0:T(8,128)(2,1)}, f32[1,96,1024]{2,1,0:T(8,128)}, bf16[1,96,32]{1,2,0:T(8,128)(2,1)S(1)}) conditional(s32[]{:T(128)} %convert_element_type.111, () %tuple.101, (bf16[96,4096]{1,0:T(8,128)(2,1)S(1)}, bf16[4096]{0:T(1024)(128)(2,1)S(1)}, bf16[4096,1024]{1,0:T(8,128)(2,1)}, bf16[4096,1024]{1,0:T(8,128)(2,1)}, ...), branch_computations={%region_1.1_spmd, %region_2.3_spmd} | conditional | flops 1641782400 | bytes 46989256 | solution.py:210
  280.3 5.8 %fusion.6 = f32[96,1024]{1,0:T(8,128)} fusion(bf16[4096,1024]{1,0:T(8,128)(2,1)} %get-tuple-element.596, bf16[96,4096]{1,0:T(8,128)(2,1)S(1)} %get-tuple-element.594, f32[4096]{0:T(1024)S(1)} %convert_element_type.61, f32[96]{0:T(128)S(1)} %add_rsqrt_fusion), kind=kOutput, calls=%fused_computation.10 | convolution fusion | flops 806879232 | bytes 9585024 | tf_op jit(solution)/shard_map/while/body/eval_jaxpr/cond/branch_1_fun/dot_general | solution.py:126
  286.1 4.6 fusion
  299.0 18.5 %collective-permute-start = (bf16[96,4096]{1,0:T(8,128)(2,1)}, bf16[96,4096]{1,0:T(8,128)(2,1)S(1)}, u32[]{:S(2)}, u32[]{:S(2)}) collective-permute-start(bf16[96,4096]{1,0:T(8,128)(2,1)} %get-tuple-element.881), channel_id=1, source_target_pairs={{0,8},{8,16},{16,24},{1,9},{9,17},{17,25},{2,10},{10,18},{18,26},{... | collective-permute-start | bytes 2359304 | tf_op jit(solution)/shard_map/while/body/eval_jaxpr/ppermute | solution.py:115
  323.0 11.4 %collective-permute-start = (bf16[96,4096]{1,0:T(8,128)(2,1)}, bf16[96,4096]{1,0:T(8,128)(2,1)S(1)}, u32[]{:S(2)}, u32[]{:S(2)}) collective-permute-start(bf16[96,4096]{1,0:T(8,128)(2,1)} %get-tuple-element.881), channel_id=1, source_target_pairs={{0,8},{8,16},{16,24},{1,9},{9,17},{17,25},{2,10},{10,18},{18,26},{... | collective-permute-start | bytes 2359304 | tf_op jit(solution)/shard_map/while/body/eval_jaxpr/ppermute | solution.py:115
  340.0 20.9 %collective-permute-start = (bf16[96,4096]{1,0:T(8,128)(2,1)}, bf16[96,4096]{1,0:T(8,128)(2,1)S(1)}, u32[]{:S(2)}, u32[]{:S(2)}) collective-permute-start(bf16[96,4096]{1,0:T(8,128)(2,1)} %get-tuple-element.881), channel_id=1, source_target_pairs={{0,8},{8,16},{16,24},{1,9},{9,17},{17,25},{2,10},{10,18},{18,26},{... | collective-permute-start | bytes 2359304 | tf_op jit(solution)/shard_map/while/body/eval_jaxpr/ppermute | solution.py:115
  363.1 101.2 %while.38 = (s32[]{:T(128)}, bf16[96,4096]{1,0:T(8,128)(2,1)S(1)}, f32[2,32,32]{2,1,0:T(8,128)S(1)}, s32[]{:T(128)}, pred[]{:T(512)}, /*index=5*/bf16[2,96,4096]...) while((s32[]{:T(128)}, bf16[96,4096]{1,0:T(8,128)(2,1)S(1)}, ...), condition=%wide.region_10.11_spmd, body=%wide.region_5.10_spmd.sunk | while | flops 1624286464 | bytes 61204156 | solution.py:278
  365.5 12.1 %collective-permute-done.1 = bf16[96,4096]{1,0:T(8,128)(2,1)S(1)} collective-permute-done((bf16[96,4096]{1,0:T(8,128)(2,1)}, bf16[96,4096]{1,0:T(8,128)(2,1)S(1)}, u32[]{:S(2)}, u32[]{:S(2)}) %collective-permute-start.1) | collective-permute-done | bytes 786464 | tf_op jit(solution)/shard_map/while/body/eval_jaxpr/ppermute | solution.py:115
  379.8 12.8 %collective-permute-done.1 = bf16[96,4096]{1,0:T(8,128)(2,1)S(1)} collective-permute-done((bf16[96,4096]{1,0:T(8,128)(2,1)}, bf16[96,4096]{1,0:T(8,128)(2,1)S(1)}, u32[]{:S(2)}, u32[]{:S(2)}) %collective-permute-start.1) | collective-permute-done | bytes 786464 | tf_op jit(solution)/shard_map/while/body/eval_jaxpr/ppermute | solution.py:115
  395.0 30.0 %collective-permute-done.1 = bf16[96,4096]{1,0:T(8,128)(2,1)S(1)} collective-permute-done((bf16[96,4096]{1,0:T(8,128)(2,1)}, bf16[96,4096]{1,0:T(8,128)(2,1)S(1)}, u32[]{:S(2)}, u32[]{:S(2)}) %collective-permute-start.1) | collective-permute-done | bytes 786464 | tf_op jit(solution)/shard_map/while/body/eval_jaxpr/ppermute | solution.py:115
  425.0 10.8 %conditional.5 = (bf16[96,4096]{1,0:T(8,128)(2,1)}, f32[1,32,32]{2,1,0:T(8,128)S(1)}) conditional(s32[]{:T(128)} %convert_element_type.112, () %tuple.104, (pred[]{:T(512)}, bf16[2,96,4096]{2,1,0:T(8,128)(2,1)}, s32[]{:T(128)}, bf16[96,4096]{1,0:T(8,128)(2,1)S(1)}, bf16[2,96,4096]{2,1,0:T(8,128)(2,1)S(1)}, /*index=5*/bf16[4096,1024]{1,0:T(8,128)(2,1)}, ...), branch_computations={%region_6.6_spmd, %region_7.9_spmd} | conditional | flops 1624285440 | bytes 58008936 | solution.py:265
  425.0 5.2 %fusion.18 = bf16[96,1024]{1,0:T(8,128)(2,1)S(1)} fusion(bf16[4096,1024]{1,0:T(8,128)(2,1)} %get-tuple-element.620, f32[2,96,1024]{2,1,0:T(8,128)S(1)} %get-tuple-element.621, s32[]{:T(128)} %get-tuple-element.617, bf16[96,4096]{1,0:T(8,128)(2,1)S(1)} %get-tuple-element.618, bf16[2,96,4096]{2,1,0:T(8,128)(2,1)} %get-tuple-element.616, pred[]{:T(512)} %get-tuple-element.615), kind=kOutput, calls=%fused_computation.31 | convolution fusion | flops 806584320 | bytes 10552832 | tf_op jit(solution)/shard_map/while/body/eval_jaxpr/cond/branch_1_fun/dot_general | solution.py:141
  437.0 12.2 %collective-permute-done.1 = bf16[96,4096]{1,0:T(8,128)(2,1)S(1)} collective-permute-done((bf16[96,4096]{1,0:T(8,128)(2,1)}, bf16[96,4096]{1,0:T(8,128)(2,1)S(1)}, u32[]{:S(2)}, u32[]{:S(2)}) %collective-permute-start.1) | collective-permute-done | bytes 786464 | tf_op jit(solution)/shard_map/while/body/eval_jaxpr/ppermute | solution.py:115
  449.2 10.8 %conditional.5 = (bf16[96,4096]{1,0:T(8,128)(2,1)}, f32[1,32,32]{2,1,0:T(8,128)S(1)}) conditional(s32[]{:T(128)} %convert_element_type.112, () %tuple.104, (pred[]{:T(512)}, bf16[2,96,4096]{2,1,0:T(8,128)(2,1)}, s32[]{:T(128)}, bf16[96,4096]{1,0:T(8,128)(2,1)S(1)}, bf16[2,96,4096]{2,1,0:T(8,128)(2,1)S(1)}, /*index=5*/bf16[4096,1024]{1,0:T(8,128)(2,1)}, ...), branch_computations={%region_6.6_spmd, %region_7.9_spmd} | conditional | flops 1624285440 | bytes 58008936 | solution.py:265
  449.2 5.2 %fusion.18 = bf16[96,1024]{1,0:T(8,128)(2,1)S(1)} fusion(bf16[4096,1024]{1,0:T(8,128)(2,1)} %get-tuple-element.620, f32[2,96,1024]{2,1,0:T(8,128)S(1)} %get-tuple-element.621, s32[]{:T(128)} %get-tuple-element.617, bf16[96,4096]{1,0:T(8,128)(2,1)S(1)} %get-tuple-element.618, bf16[2,96,4096]{2,1,0:T(8,128)(2,1)} %get-tuple-element.616, pred[]{:T(512)} %get-tuple-element.615), kind=kOutput, calls=%fused_computation.31 | convolution fusion | flops 806584320 | bytes 10552832 | tf_op jit(solution)/shard_map/while/body/eval_jaxpr/cond/branch_1_fun/dot_general | solution.py:141
  464.5 30.5 %all-gather = f32[8,2,1024]{2,1,0:T(2,128)S(1)} all-gather(f32[1,2,1024]{2,1,0:T(2,128)S(1)} %reshape.67), channel_id=1, replica_groups=mesh['section'=4,'dp'=8] {'dp'}, dimensions={0}, use_global_device_ids=true | all-gather | bytes 73728 | tf_op jit(solution)/shard_map/all_gather | solution.py:280
  497.2 3.9 all_scores.1
  501.2 12.9 %psum.7 = f32[2,16]{1,0:T(2,128)} all-reduce(f32[2,16]{1,0:T(2,128)S(1)} %constant_dynamic-slice_fusion), channel_id=1, replica_groups=mesh['section'=4,'dp'=8] {'section'}, use_global_device_ids=true, to_apply=%region_11.12 | all-reduce | flops 32 | bytes 256 | tf_op jit(solution)/shard_map/psum | solution.py:285
  (140 shorter events, 70.6 us)
Async XLA Ops:
  6.5 178.8 %all-gather.4.cloned.1.call-start = ((), (), s32[]{:S(2)}) async-start(), calls=%async_computation | async-start | bytes 9437184 | tf_op jit(solution)/shard_map/all_gather | solution.py:172
  7.3 254.4 %all-gather.6.cloned.1.call-start = ((), (), s32[]{:S(2)}) async-start(), calls=%async_computation.1 | async-start | bytes 9437184 | tf_op jit(solution)/shard_map/all_gather | solution.py:173
  262.0 101.1 %copy-start.5 = (bf16[1,32,1024]{2,1,0:T(8,128)(2,1)S(1)}, bf16[1,32,1024]{2,1,0:T(8,128)(2,1)}, u32[]{:S(2)}) copy-start(bf16[1,32,1024]{2,1,0:T(8,128)(2,1)} %param.26) | copy-start | bytes 196612
  263.7 6.1 %slice-start = ((s8[8388608]{0:T(1024)(128)(4,1)}), s8[4194304]{0:T(1024)(128)(4,1)S(1)}, s32[]{:S(2)}) async-start(s8[8388608]{0:T(1024)(128)(4,1)} %bitcast.61), calls=%async_computation.2 | async-start | bytes 8388608 | tf_op jit(solution)/shard_map/while/body/eval_jaxpr/cond
  264.0 5.8 %slice-start.1 = ((s8[8388608]{0:T(1024)(128)(4,1)}), s8[4194304]{0:T(1024)(128)(4,1)S(1)}, s32[]{:S(2)}) async-start(s8[8388608]{0:T(1024)(128)(4,1)} %bitcast.61), calls=%async_computation.3 | async-start | bytes 8388608 | tf_op jit(solution)/shard_map/while/body/eval_jaxpr/cond
  274.9 3.4 collective-permute-start
  280.0 6.1 %slice-start = ((s8[8388608]{0:T(1024)(128)(4,1)}), s8[4194304]{0:T(1024)(128)(4,1)S(1)}, s32[]{:S(2)}) async-start(s8[8388608]{0:T(1024)(128)(4,1)} %bitcast.61), calls=%async_computation.2 | async-start | bytes 8388608 | tf_op jit(solution)/shard_map/while/body/eval_jaxpr/cond
  280.3 5.8 %slice-start.1 = ((s8[8388608]{0:T(1024)(128)(4,1)}), s8[4194304]{0:T(1024)(128)(4,1)S(1)}, s32[]{:S(2)}) async-start(s8[8388608]{0:T(1024)(128)(4,1)} %bitcast.61), calls=%async_computation.3 | async-start | bytes 8388608 | tf_op jit(solution)/shard_map/while/body/eval_jaxpr/cond
  291.2 4.4 collective-permute-start
  299.0 20.6 %collective-permute-start = (bf16[96,4096]{1,0:T(8,128)(2,1)}, bf16[96,4096]{1,0:T(8,128)(2,1)S(1)}, u32[]{:S(2)}, u32[]{:S(2)}) collective-permute-start(bf16[96,4096]{1,0:T(8,128)(2,1)} %get-tuple-element.881), channel_id=1, source_target_pairs={{0,8},{8,16},{16,24},{1,9},{9,17},{17,25},{2,10},{10,18},{18,26},{... | collective-permute-start | bytes 2359304 | tf_op jit(solution)/shard_map/while/body/eval_jaxpr/ppermute | solution.py:115
  323.0 13.5 %collective-permute-start = (bf16[96,4096]{1,0:T(8,128)(2,1)}, bf16[96,4096]{1,0:T(8,128)(2,1)S(1)}, u32[]{:S(2)}, u32[]{:S(2)}) collective-permute-start(bf16[96,4096]{1,0:T(8,128)(2,1)} %get-tuple-element.881), channel_id=1, source_target_pairs={{0,8},{8,16},{16,24},{1,9},{9,17},{17,25},{2,10},{10,18},{18,26},{... | collective-permute-start | bytes 2359304 | tf_op jit(solution)/shard_map/while/body/eval_jaxpr/ppermute | solution.py:115
  340.0 22.9 %collective-permute-start = (bf16[96,4096]{1,0:T(8,128)(2,1)}, bf16[96,4096]{1,0:T(8,128)(2,1)S(1)}, u32[]{:S(2)}, u32[]{:S(2)}) collective-permute-start(bf16[96,4096]{1,0:T(8,128)(2,1)} %get-tuple-element.881), channel_id=1, source_target_pairs={{0,8},{8,16},{16,24},{1,9},{9,17},{17,25},{2,10},{10,18},{18,26},{... | collective-permute-start | bytes 2359304 | tf_op jit(solution)/shard_map/while/body/eval_jaxpr/ppermute | solution.py:115
  363.1 131.9 %copy-start.2 = (s32[16]{0:T(128)S(1)}, s32[16]{0:T(128)}, u32[]{:S(2)}) copy-start(s32[16]{0:T(128)} %param.21) | copy-start | bytes 196
  364.2 13.4 %collective-permute-start.1 = (bf16[96,4096]{1,0:T(8,128)(2,1)}, bf16[96,4096]{1,0:T(8,128)(2,1)S(1)}, u32[]{:S(2)}, u32[]{:S(2)}) collective-permute-start(bf16[96,4096]{1,0:T(8,128)(2,1)} %get-tuple-element.898), channel_id=1, source_target_pairs={{8,0},{16,8},{24,16},{9,1},{17,9},{25,17},{10,2},{18,10},{26,18},{... | collective-permute-start | bytes 2359304 | tf_op jit(solution)/shard_map/while/body/eval_jaxpr/ppermute | solution.py:115
  378.5 14.1 %collective-permute-start.1 = (bf16[96,4096]{1,0:T(8,128)(2,1)}, bf16[96,4096]{1,0:T(8,128)(2,1)S(1)}, u32[]{:S(2)}, u32[]{:S(2)}) collective-permute-start(bf16[96,4096]{1,0:T(8,128)(2,1)} %get-tuple-element.898), channel_id=1, source_target_pairs={{8,0},{16,8},{24,16},{9,1},{17,9},{25,17},{10,2},{18,10},{26,18},{... | collective-permute-start | bytes 2359304 | tf_op jit(solution)/shard_map/while/body/eval_jaxpr/ppermute | solution.py:115
  393.7 31.3 %collective-permute-start.1 = (bf16[96,4096]{1,0:T(8,128)(2,1)}, bf16[96,4096]{1,0:T(8,128)(2,1)S(1)}, u32[]{:S(2)}, u32[]{:S(2)}) collective-permute-start(bf16[96,4096]{1,0:T(8,128)(2,1)} %get-tuple-element.898), channel_id=1, source_target_pairs={{8,0},{16,8},{24,16},{9,1},{17,9},{25,17},{10,2},{18,10},{26,18},{... | collective-permute-start | bytes 2359304 | tf_op jit(solution)/shard_map/while/body/eval_jaxpr/ppermute | solution.py:115
  425.0 5.2 %slice-start.2 = ((s8[8388608]{0:T(1024)(128)(4,1)}), s8[4194304]{0:T(1024)(128)(4,1)S(1)}, s32[]{:S(2)}) async-start(s8[8388608]{0:T(1024)(128)(4,1)} %bitcast.64), calls=%async_computation.4 | async-start | bytes 8388608 | tf_op jit(solution)/shard_map/while/body/eval_jaxpr/cond
  425.0 6.1 %slice-start.3 = ((s8[8388608]{0:T(1024)(128)(4,1)}), s8[4194304]{0:T(1024)(128)(4,1)S(1)}, s32[]{:S(2)}) async-start(s8[8388608]{0:T(1024)(128)(4,1)} %bitcast.64), calls=%async_computation.5 | async-start | bytes 8388608 | tf_op jit(solution)/shard_map/while/body/eval_jaxpr/cond
  431.0 2.8 copy-start.4
  435.7 13.5 %collective-permute-start.1 = (bf16[96,4096]{1,0:T(8,128)(2,1)}, bf16[96,4096]{1,0:T(8,128)(2,1)S(1)}, u32[]{:S(2)}, u32[]{:S(2)}) collective-permute-start(bf16[96,4096]{1,0:T(8,128)(2,1)} %get-tuple-element.898), channel_id=1, source_target_pairs={{8,0},{16,8},{24,16},{9,1},{17,9},{25,17},{10,2},{18,10},{26,18},{... | collective-permute-start | bytes 2359304 | tf_op jit(solution)/shard_map/while/body/eval_jaxpr/ppermute | solution.py:115
  449.2 5.2 %slice-start.2 = ((s8[8388608]{0:T(1024)(128)(4,1)}), s8[4194304]{0:T(1024)(128)(4,1)S(1)}, s32[]{:S(2)}) async-start(s8[8388608]{0:T(1024)(128)(4,1)} %bitcast.64), calls=%async_computation.4 | async-start | bytes 8388608 | tf_op jit(solution)/shard_map/while/body/eval_jaxpr/cond
  449.2 6.1 %slice-start.3 = ((s8[8388608]{0:T(1024)(128)(4,1)}), s8[4194304]{0:T(1024)(128)(4,1)S(1)}, s32[]{:S(2)}) async-start(s8[8388608]{0:T(1024)(128)(4,1)} %bitcast.64), calls=%async_computation.5 | async-start | bytes 8388608 | tf_op jit(solution)/shard_map/while/body/eval_jaxpr/cond
  455.3 2.8 copy-start.4
  460.0 4.4 collective-permute-start.1
  (11 other events, 19.2 us)
Sparse Core Ops, SparseCore 0:
  9.5 127.1 all-gather.3
  138.8 122.8 all-gather.5

commit v2 on v1

v2 whole, which is shorter than its diff:
```python
import functools

import jax
import jax.numpy as jnp
from jax import lax
from jax.experimental import pallas as pl
from jax.experimental.pallas import tpu as pltpu
from jax.sharding import PartitionSpec as P


HIGHEST = lax.Precision.HIGHEST


def inverted(block):
    size = block.shape[0]
    rows = lax.broadcasted_iota(jnp.int32, block.shape, 0)
    columns = lax.broadcasted_iota(jnp.int32, block.shape, 1)

    def sweep(pivot, held):
        at_row, at_column = rows == pivot, columns == pivot
        row = jnp.sum(jnp.where(at_row, held, 0.0), axis=0, keepdims=True)
        column = jnp.sum(jnp.where(at_column, held, 0.0), axis=1, keepdims=True)
        corner = jnp.sum(jnp.where(at_column[:1], row, 0.0), axis=1, keepdims=True)
        scale = 1.0 / corner
        scaled = row * scale
        updated = held - column * scaled
        updated = jnp.where(at_row, scaled, updated)
        updated = jnp.where(at_column, column * scale, updated)
        return jnp.where(at_row & at_column, -scale, updated)

    return -lax.fori_loop(0, size, sweep, block)


def invert_in_place(work, strip, block):
    size = work.shape[0]
    count = size // block

    def eliminate(step, carry):
        span = pl.ds(pl.multiple_of(step * block, block), block)
        corner = inverted(work[span, span])
        strip[...] = jnp.dot(
            corner, work[span, :], precision=HIGHEST, preferred_element_type=jnp.float32
        )

        def update(other, carry):
            across = pl.ds(pl.multiple_of(other * block, block), block)
            lead = work[span, across].T

            @pl.when(other != step)
            def _():
                work[across, :] -= jnp.dot(
                    lead, strip[...], precision=HIGHEST, preferred_element_type=jnp.float32
                )
                work[across, span] = strip[:, across].T

            return carry

        lax.fori_loop(0, count, update, 0)
        work[span, :] = strip[...]
        work[span, span] = -corner
        return carry

    lax.fori_loop(0, count, eliminate, 0)


def prior_kernel(prior, work, strip):
    work[...] = prior[...]
    invert_in_place(work, strip, strip.shape[0])


def prior_inverse(prior):
    size = prior.shape[0]
    block = 128
    return pl.pallas_call(
        prior_kernel,
        out_shape=jax.ShapeDtypeStruct((size, size), jnp.float32),
        in_specs=[pl.BlockSpec(memory_space=pltpu.VMEM)],
        out_specs=pl.BlockSpec(memory_space=pltpu.VMEM),
        scratch_shapes=[pltpu.VMEM((block, size), jnp.float32)],
        compiler_params=pltpu.CompilerParams(vmem_limit_bytes=24 * 2**20),
        cost_estimate=pl.CostEstimate(flops=10**11, bytes_accessed=8 * size * size, transcendentals=0),
        name="prior_inverse",
    )(prior)


def score_kernel(everyone, negated, queries, out):
    grads = everyone[...]
    half = jnp.dot(grads, negated[...], precision=HIGHEST, preferred_element_type=jnp.float32)
    gram = -lax.dot_general(
        half, grads, (((1,), (1,)), ((), ())), precision=HIGHEST,
        preferred_element_type=jnp.float32,
    )
    count = grads.shape[0]
    rows = lax.broadcasted_iota(jnp.int32, (count, count), 0)
    columns = lax.broadcasted_iota(jnp.int32, (count, count), 1)
    inverse = inverted(gram + jnp.where(rows == columns, 1.0, 0.0))
    full = jnp.dot(gram, inverse, precision=HIGHEST, preferred_element_type=jnp.float32)
    owners = lax.broadcasted_iota(jnp.int32, (count, queries.shape[1]), 0)
    selector = jnp.where(owners == queries[...], 1.0, 0.0)
    out[...] = jnp.dot(full, selector, precision=HIGHEST, preferred_element_type=jnp.float32)


def all_scores(everyone, negated, queries):
    return pl.pallas_call(
        score_kernel,
        out_shape=jax.ShapeDtypeStruct((everyone.shape[0], queries.shape[0]), jnp.float32),
        in_specs=[pl.BlockSpec(memory_space=pltpu.VMEM)] * 3,
        out_specs=pl.BlockSpec(memory_space=pltpu.VMEM),
        compiler_params=pltpu.CompilerParams(vmem_limit_bytes=24 * 2**20),
        name="all_scores",
    )(everyone, negated, queries[None, :])


MESH = pl.DeviceIdType.MESH
CONTRACT_LAST = (((1,), (1,)), ((), ()))


def relay_kernel(
    sections, batches, example_rows,
    inputs, targets, gain, value_map, output_map, input_map, output_map_small,
    grads,
    hidden, following, cotangent, previous, values, normed, activated, features, factors,
    forward_send, forward_receive, backward_send, backward_receive,
):
    me = lax.axis_index("section")
    has_before, has_after = me > 0, me < sections - 1
    before, after = lax.max(me - 1, 0), lax.min(me + 1, sections - 1)
    width, value_width = value_map.shape
    signal_width = output_map_small.shape[0]
    chunks = forward_send.shape[1]
    chunk = width // chunks
    tile = 256
    group = 16

    def span(index, size):
        return pl.ds(pl.multiple_of(index * size, size), size)

    def forward_copy(batch, piece):
        columns = span(piece, chunk)
        return pltpu.make_async_remote_copy(
            src_ref=following.at[batch, :, columns],
            dst_ref=hidden.at[batch, :, columns],
            send_sem=forward_send.at[batch, piece],
            recv_sem=forward_receive.at[batch, piece],
            device_id={"section": after},
            device_id_type=MESH,
        )

    def backward_copy(batch, piece):
        columns = span(piece, chunk)
        return pltpu.make_async_remote_copy(
            src_ref=previous.at[batch, :, columns],
            dst_ref=cotangent.at[batch, :, columns],
            send_sem=backward_send.at[batch, piece],
            recv_sem=backward_receive.at[batch, piece],
            device_id={"section": before},
            device_id_type=MESH,
        )

    barrier = pltpu.get_barrier_semaphore()

    @pl.when(has_before)
    def _():
        pl.semaphore_signal(barrier, inc=1, device_id={"section": before}, device_id_type=MESH)

    @pl.when(has_after)
    def _():
        pl.semaphore_signal(barrier, inc=1, device_id={"section": after}, device_id_type=MESH)

    peers = lax.min(me, 1) + lax.min(sections - 1 - me, 1)
    pl.semaphore_wait(barrier, peers)

    @pl.loop(0, batches)
    def _(batch):
        @pl.when(has_before)
        def _():
            @pl.loop(0, chunks)
            def _(piece):
                forward_copy(batch, piece).wait_recv()

        @pl.when(jnp.logical_not(has_before))
        def _():
            hidden[batch] = inputs[batch]

        @pl.loop(0, example_rows // group)
        def _(at):
            rows = span(at, group)
            widened = hidden[batch, rows, :].astype(jnp.float32)
            factor = lax.rsqrt(jnp.mean(widened * widened, axis=-1, keepdims=True) + 1e-05)
            factors[batch, rows, :] = factor
            normed[rows, :] = (widened * factor * gain[...]).astype(jnp.bfloat16)

        @pl.loop(0, value_width // tile)
        def _(at):
            columns = span(at, tile)
            found = jnp.dot(
                normed[...], value_map[:, columns], preferred_element_type=jnp.float32
            )
            values[batch, :, columns] = found
            activated[:, columns] = (found / (1.0 + jnp.exp(-found))).astype(jnp.bfloat16)

        @pl.when(has_after)
        def _():
            @pl.loop(0, chunks)
            def _(piece):
                columns = span(piece, chunk)
                branch = lax.dot_general(
                    activated[...], output_map[columns, :], CONTRACT_LAST,
                    preferred_element_type=jnp.float32,
                )
                following[batch, :, columns] = (
                    hidden[batch, :, columns].astype(jnp.float32) + branch
                ).astype(jnp.bfloat16)
                forward_copy(batch, piece).start()

        features[batch] = lax.dot_general(
            normed[...], input_map[...], CONTRACT_LAST, preferred_element_type=jnp.float32
        ).astype(jnp.bfloat16)

    @pl.loop(0, batches)
    def _(batch):
        @pl.when(has_after)
        def _():
            @pl.loop(0, chunks)
            def _(piece):
                backward_copy(batch, piece).wait_recv()

        @pl.when(jnp.logical_not(has_after))
        def _():
            cotangent[batch] = targets[batch]

        slopes = activated

        def upstream_tile(at, total):
            columns = span(at, tile)
            upstream = jnp.dot(
                cotangent[batch], output_map[:, columns], preferred_element_type=jnp.float32
            )
            found = values[batch, :, columns]
            logistic = 1.0 / (1.0 + jnp.exp(-found))
            slope = (upstream * logistic * (1.0 + found * (1.0 - logistic))).astype(jnp.bfloat16)
            slopes[:, columns] = slope
            return total + jnp.sum(slope.astype(jnp.float32) * found, axis=-1, keepdims=True)

        total = lax.fori_loop(
            0, value_width // tile, upstream_tile, jnp.zeros((example_rows, 1), jnp.float32)
        )
        factor = factors[batch]
        shrink = total * (factor * factor) * (1.0 / width)

        @pl.when(has_before)
        def _():
            @pl.loop(0, chunks)
            def _(piece):
                columns = span(piece, chunk)
                normed_grad = lax.dot_general(
                    slopes[...], value_map[columns, :], CONTRACT_LAST,
                    preferred_element_type=jnp.float32,
                )
                weighted = normed_grad * gain[:, columns]
                hidden_grad = (
                    factor * weighted - hidden[batch, :, columns].astype(jnp.float32) * shrink
                )
                previous[batch, :, columns] = (
                    cotangent[batch, :, columns].astype(jnp.float32) + hidden_grad
                ).astype(jnp.bfloat16)
                backward_copy(batch, piece).start()

        signals = lax.dot_general(
            slopes[...], output_map_small[...], CONTRACT_LAST, preferred_element_type=jnp.float32
        ).astype(jnp.bfloat16)
        grads[batch] = lax.dot_general(
            signals, features[batch], (((0,), (0,)), ((), ())), preferred_element_type=jnp.float32
        ) * (1.0 / example_rows)

    @pl.loop(0, batches)
    def _(batch):
        @pl.loop(0, chunks)
        def _(piece):
            @pl.when(has_after)
            def _():
                forward_copy(batch, piece).wait_send()

            @pl.when(has_before)
            def _():
                backward_copy(batch, piece).wait_send()


def relay(inputs, targets, gain, value_map, output_map, input_map, output_map_small):
    batches, example_rows, width = inputs.shape
    value_width = value_map.shape[1]
    feature_width = input_map.shape[0]
    signal_width = output_map_small.shape[0]
    chunks = 8
    stream = pltpu.VMEM((batches, example_rows, width), jnp.bfloat16)
    return pl.pallas_call(
        functools.partial(relay_kernel, lax.axis_size("section"), batches, example_rows),
        out_shape=jax.ShapeDtypeStruct((batches, signal_width, feature_width), jnp.float32),
        in_specs=[pl.BlockSpec(memory_space=pltpu.VMEM)] * 7,
        out_specs=pl.BlockSpec(memory_space=pltpu.VMEM),
        scratch_shapes=[
            stream, stream, stream, stream,
            pltpu.VMEM((batches, example_rows, value_width), jnp.float32),
            pltpu.VMEM((example_rows, width), jnp.bfloat16),
            pltpu.VMEM((example_rows, value_width), jnp.bfloat16),
            pltpu.VMEM((batches, example_rows, feature_width), jnp.bfloat16),
            pltpu.VMEM((batches, example_rows, 1), jnp.float32),
        ] + [pltpu.SemaphoreType.DMA((batches, chunks))] * 4,
        compiler_params=pltpu.CompilerParams(
            collective_id=1, has_side_effects=True, vmem_limit_bytes=48 * 2**20
        ),
        name="relay",
    )(inputs, targets, gain, value_map, output_map, input_map, output_map_small)


def per_device(
    inputs,
    output_cotangent,
    lengths,
    query_examples,
    norm_gain,
    value_weight,
    output_weight,
    input_projection,
    output_projection,
    fisher_prior,
):
    value_map, output_map = (
        lax.all_gather(value_weight, "dp", axis=1, tiled=True),
        lax.all_gather(output_weight, "dp", axis=1, tiled=True),
    )
    value_map = value_map[0]
    output_map = output_map[0]
    gain = norm_gain.astype(jnp.float32)
    input_map = input_projection[0]
    output_map_small = output_projection[0]
    negated_inverse = prior_inverse(fisher_prior[0])
    batches = lengths.shape[0]
    example_rows = inputs.shape[0] // batches
    width = inputs.shape[1]
    feature_width = input_map.shape[0]
    signal_width = output_map_small.shape[0]
    entries = inputs.reshape(batches, example_rows, width)
    positions = jnp.arange(example_rows, dtype=jnp.int32)
    keep = (positions[None, :] < lengths[:, None]).astype(jnp.bfloat16)
    targets = output_cotangent.reshape(batches, example_rows, width) * keep[:, :, None]
    saved_grads = relay(
        entries, targets, gain, value_map, output_map, input_map, output_map_small
    )
    flat = saved_grads.reshape(batches, signal_width * feature_width)
    everyone = lax.all_gather(flat, "dp", axis=0, tiled=True)
    every_score = all_scores(everyone, negated_inverse, query_examples)
    section_scores = lax.dynamic_slice_in_dim(
        every_score, lax.axis_index("dp") * batches, batches, 0
    )
    return lax.psum(section_scores, "section")


def solution(mesh):
    placed = (
        P("dp", None),
        P("dp", None),
        P("dp"),
        P(),
        P("section", None),
        P("section", "dp", None),
        P("section", "dp", None),
        P("section", None, None),
        P("section", None, None),
        P("section", None, None),
    )
    return jax.shard_map(
        per_device, mesh=mesh, in_specs=placed, out_specs=P("dp", None), check_vma=False
    )
```

time: 522 us -> 399 us (0.76)
  Pallas kernels: 176 us -> 263 us
  waiting for transfers between devices: 156 us -> 79 us
  starting transfers between devices: 61 us -> 0.04 us
  matrix products: 38.5 us -> 0 us
  other arithmetic: 15.7 us -> 0.26 us
  local copies, waits for them, and re-layouts: 17 us -> 6.46 us
  blocking collectives: 43.4 us -> 36.9 us
    pallas_call x0 -> x1, Pallas kernels: none -> 87 us  [relay(): pl.pallas_call(functools.partial(relay_kernel, lax.axis_size('section'),...]
    ppermute x10 -> x0, waiting for transfers between devices: 77.9 us -> none  [shifted(): lax.ppermute(value, axis, [(source, source + steps) for source in range(f...]
    ppermute x10 -> x0, starting transfers between devices: 61 us -> none  [shifted(): lax.ppermute(value, axis, [(source, source + steps) for source in range(f...]
    dot_general x12 -> x0, matrix products: 38.5 us -> none  [the longest x2 11.6 us: forward_block(): values = jnp.dot(normed, value_map, preferred_element_type=jnp.float32)]
    select_n x20 -> x0, other arithmetic: 10.6 us -> none  [the longest x5 8.09 us: forward_tick(): jnp.where(active, lax.dynamic_update_index_in_dim(saved_hidden, hidden, p...]
    psum x1, blocking collectives: 12.9 us -> 6.31 us  [per_device(): return lax.psum(section_scores, 'section')]
    another operation x8 -> x0, local copies, waits for them, and re-layouts: 6.04 us -> none
  transfers between devices with their start and end apart: 12 -> 2, of which waited for: 11 -> 1; matrix products, arithmetic and copies ran while one was open for 1% -> 0% of each run, Pallas kernels for 33% -> 43%
where the time goes in v2:
time: 399 us
  Pallas kernels  263 us (66%)
  waiting for transfers between devices  79 us (20%)
  blocking collectives  36.9 us (9%)
  between operations  13.5 us (3%)
  local copies, waits for them, and re-layouts  6.46 us (2%)
    pallas_call x1, Pallas kernels, prior_inverse(): pl.pallas_call(prior_kernel, out_shape=jax.ShapeDtypeStruct((size, size),...  172 us
    pallas_call x1, Pallas kernels, relay(): pl.pallas_call(functools.partial(relay_kernel, lax.axis_size('section'),...  87 us
    all_gather x1, waiting for transfers between devices, per_device(): lax.all_gather(output_weight, 'dp', axis=1, tiled=True)  77.6 us
    all_gather x1, blocking collectives, per_device(): everyone = lax.all_gather(flat, 'dp', axis=0, tiled=True)  30.5 us
  transfers between devices with their start and end apart: 2, of which 1 were waited for; matrix products, arithmetic and copies ran while one was open for 0% of the time, Pallas kernels for 43%

profile of v2, /device:TPU:0, one launch (start us, length us, event | category | flops | bytes accessed | tf_op | source)
XLA Modules:
  0.0 398.7 jit_solution(14028101850398235703)
XLA Ops:
  6.5 0.0 all-gather.4.cloned.1.call-start
  6.5 0.7 all-gather.4.cloned.1.call-update
  7.3 0.0 all-gather.6.cloned.1.call-start
  7.3 0.7 all-gather.6.cloned.1.call-update
  8.0 0.0 copy-done.8
  8.1 0.0 copy-done.9
  8.1 0.1 compare_convert_fusion
  8.1 0.0 copy-done.7
  8.1 0.2 broadcast_multiply_fusion.targets
  8.3 0.0 copy-start.6
  8.3 2.2 copy-done.6
  10.5 171.7 %prior_inverse.1.negated = f32[1024,1024]{1,0:T(8,128)S(1)} custom-call(f32[1024,1024]{1,0:T(8,128)S(1)} %bitcast.12), custom_call_target="tpu_custom_call" | custom-call | flops 99999997952 | bytes 8388608 | tf_op jit(solution)/shard_map/prior_inverse/pallas_call | solution.py:74
  182.2 0.0 copy-start
  182.2 1.9 copy-done
  184.1 77.6 %all-gather.6.cloned.1.call-done = bf16[1,4096,1024]{2,1,0:T(8,128)(2,1)} async-done(((bf16[1,512,1024]{2,1,0:T(8,128)(2,1)}), bf16[1,4096,1024]{2,1,0:T(8,128)(2,1)}) %all-gather.6.cloned.1.call-update) | async-done | bytes 8388624 | tf_op jit(solution)/shard_map/all_gather | solution.py:330
  261.7 0.0 copy-done.2
  261.7 0.0 copy-done.3
  261.7 0.0 copy-done.4
  261.7 87.0 %relay.1 = f32[2,32,32]{2,1,0:T(8,128)S(1)} custom-call(bf16[2,96,4096]{2,1,0:T(8,128)(2,1)S(1)} %bitcast.8, bf16[2,96,4096]{2,1,0:T(8,128)(2,1)S(1)} %broadcast_multiply_fusion.targets, f32[1,4096]{1,0:T(1,128)S(1)} %convert_element_type.11.gain, bf16[4096,1024]{1,0:T(8,128)(2,1)} %bitcast.13, bf16[4096,1024]{1,0:T(8,128)(2,1)} %bitcast.14, ...), custom_call_target="tpu_custom_call" | custom-call | tf_op jit(solution)/shard_map/relay/pallas_call | solution.py:296
  348.8 0.1 reshape.34
  348.9 30.5 %all-gather = f32[8,2,1024]{2,1,0:T(2,128)S(1)} all-gather(f32[1,2,1024]{2,1,0:T(2,128)S(1)} %reshape.34), channel_id=1, replica_groups=mesh['section'=4,'dp'=8] {'dp'}, dimensions={0}, use_global_device_ids=true | all-gather | bytes 73728 | tf_op jit(solution)/shard_map/all_gather | solution.py:351
  379.5 2.2 copy-done.1
  381.6 3.9 all_scores.1
  385.6 6.3 %psum.7 = f32[2,16]{1,0:T(2,128)} all-reduce(f32[2,16]{1,0:T(2,128)S(1)} %constant_dynamic-slice_fusion), channel_id=1, replica_groups=mesh['section'=4,'dp'=8] {'section'}, use_global_device_ids=true, to_apply=%region_0.0 | all-reduce | flops 32 | bytes 256 | tf_op jit(solution)/shard_map/psum | solution.py:356
  (13 shorter events, 0.1 us)
Async XLA Ops:
  6.5 1.5 copy-start.8
  6.5 1.5 copy-start.9
  6.5 1.6 copy-start.7
  6.5 177.6 %all-gather.4.cloned.1.call-start = ((), (), s32[]{:S(2)}) async-start(), calls=%async_computation | async-start | bytes 9437184 | tf_op jit(solution)/shard_map/all_gather | solution.py:329
  7.3 254.5 %all-gather.6.cloned.1.call-start = ((), (), s32[]{:S(2)}) async-start(), calls=%async_computation.1 | async-start | bytes 9437184 | tf_op jit(solution)/shard_map/all_gather | solution.py:330
  8.3 2.2 copy-start.6
  10.5 251.2 %copy-start.2 = (bf16[192,4096]{1,0:T(8,128)(2,1)S(1)}, bf16[192,4096]{1,0:T(8,128)(2,1)}, u32[]{:S(2)}) copy-start(bf16[192,4096]{1,0:T(8,128)(2,1)} %param.10) | copy-start | bytes 4718596
  10.5 251.2 %copy-start.3 = (bf16[1,32,4096]{2,1,0:T(8,128)(2,1)S(1)}, bf16[1,32,4096]{2,1,0:T(8,128)(2,1)}, u32[]{:S(2)}) copy-start(bf16[1,32,4096]{2,1,0:T(8,128)(2,1)} %param.17) | copy-start | bytes 786436
  10.5 251.2 %copy-start.4 = (bf16[1,32,1024]{2,1,0:T(8,128)(2,1)S(1)}, bf16[1,32,1024]{2,1,0:T(8,128)(2,1)}, u32[]{:S(2)}) copy-start(bf16[1,32,1024]{2,1,0:T(8,128)(2,1)} %param.18) | copy-start | bytes 196612
  182.2 1.9 copy-start
  261.7 117.7 %copy-start.5 = (s32[16]{0:T(128)S(1)}, s32[16]{0:T(128)}, u32[]{:S(2)}) copy-start(s32[16]{0:T(128)} %param.13) | copy-start | bytes 196
  379.5 2.2 copy-start.1
Sparse Core Ops, SparseCore 0:
  9.5 127.2 all-gather.3
  138.9 122.7 all-gather.5

commit v3 on v2

--- a/solution.py
+++ b/solution.py
@@ -31,56 +31,167 @@
     return -lax.fori_loop(0, size, sweep, block)
 
 
-def invert_in_place(work, strip, block):
-    size = work.shape[0]
-    count = size // block
-
-    def eliminate(step, carry):
-        span = pl.ds(pl.multiple_of(step * block, block), block)
-        corner = inverted(work[span, span])
-        strip[...] = jnp.dot(
-            corner, work[span, :], precision=HIGHEST, preferred_element_type=jnp.float32
+def sweep_strip(work, strip, step, block):
+    span = pl.ds(pl.multiple_of(step * block, block), block)
+    corner = inverted(work[span, span])
+    strip[...] = jnp.dot(
+        corner, work[span, :], precision=HIGHEST, preferred_element_type=jnp.float32
+    )
+    strip[:, span] = -corner
+
+
+def sweep_rest(work, strip, step, block):
+    span = pl.ds(pl.multiple_of(step * block, block), block)
+
+    @pl.loop(0, work.shape[0] // block)
+    def _(other):
+        across = pl.ds(pl.multiple_of(other * block, block), block)
+
+        @pl.when(other != step)
+        def _():
+            work[across, :] -= jnp.dot(
+                work[span, across].T, strip[...], precision=HIGHEST,
+                preferred_element_type=jnp.float32,
+            )
+            work[across, span] = strip[:, across].T
+
+    work[span, :] = strip[...]
+
+
+def ring_device(place, count):
+    if count % 4 or count < 8:
+        return place
+    fast = count // 4
+    inner = lax.min(place, 1) * lax.min(lax.max(4 * (fast - 1) + 1 - place, 0), 1)
+    along = lax.max(place - 1, 0)
+    row, step = lax.div(along, fast - 1), lax.rem(along, fast - 1)
+    odd = lax.rem(row, 2)
+    column = 1 + (1 - odd) * step + odd * (fast - 2 - step)
+    return inner * (row * fast + column) + (1 - inner) * lax.rem(count - place, count) * fast
+
+
+def ring_place(device, count):
+    if count % 4 or count < 8:
+        return device
+    fast = count // 4
+    row, column = lax.div(device, fast), lax.rem(device, fast)
+    inner = lax.min(column, 1)
+    odd = lax.rem(row, 2)
+    within = 1 + row * (fast - 1) + (1 - odd) * (column - 1) + odd * (fast - 1 - column)
+    return inner * within + (1 - inner) * lax.rem(count - row, count)
+
+
+def gather_kernel(
+    count, value_shard, output_shard, prior, value_all, output_all, work, strip,
+    send, receive, own,
+):
+    me = lax.axis_index("dp")
+    place = ring_place(me, count)
+    targets = [
+        ring_device(lax.rem(place + 1, count), count),
+        ring_device(lax.rem(place + count - 1, count), count),
+    ]
+    shards, wholes = (value_shard, output_shard), (value_all, output_all)
+    rows = value_shard.shape[0]
+    half = rows // 2
+
+    def piece(way, array, step, first):
+        back = count - step if way == 0 else step
+        origin = ring_device(lax.rem(place + back, count), count)
+        start = pl.multiple_of(origin * rows + way * half, half)
+        there = wholes[array].at[pl.ds(start, half), :]
+        here = shards[array].at[pl.ds(way * half, half), :] if first else there
+        return pltpu.make_async_remote_copy(
+            src_ref=here,
+            dst_ref=there,
+            send_sem=send.at[way, array, step],
+            recv_sem=receive.at[way, array, step],
+            device_id={"dp": targets[way]},
+            device_id_type=pl.DeviceIdType.MESH,
         )
 
-        def update(other, carry):
-            across = pl.ds(pl.multiple_of(other * block, block), block)
-            lead = work[span, across].T
-
-            @pl.when(other != step)
+    barrier = pltpu.get_barrier_semaphore()
+    for target in targets:
+        pl.semaphore_signal(
+            barrier, inc=1, device_id={"dp": target}, device_id_type=pl.DeviceIdType.MESH
+        )
+    pl.semaphore_wait(barrier, 2)
+    for array in range(2):
+        for way in range(2):
+            piece(way, array, 0, True).start()
+    mine = pl.ds(pl.multiple_of(me * rows, rows), rows)
+    kept = [
+        pltpu.make_async_copy(shards[array], wholes[array].at[mine, :], own.at[array])
+        for array in range(2)
+    ]
+    for copy in kept:
+        copy.start()
+    work[...] = prior[...]
+    block = strip.shape[0]
+    blocks = work.shape[0] // block
+
+    def pass_on(array, step):
+        for way in range(2):
+            piece(way, array, step, False).wait_recv()
+
+            @pl.when(step < count - 2)
             def _():
-                work[across, :] -= jnp.dot(
-                    lead, strip[...], precision=HIGHEST, preferred_element_type=jnp.float32
-                )
-                work[across, span] = strip[:, across].T
-
-            return carry
-
-        lax.fori_loop(0, count, update, 0)
-        work[span, :] = strip[...]
-        work[span, span] = -corner
-        return carry
-
-    lax.fori_loop(0, count, eliminate, 0)
-
-
-def prior_kernel(prior, work, strip):
-    work[...] = prior[...]
-    invert_in_place(work, strip, strip.shape[0])
-
-
-def prior_inverse(prior):
+                piece(way, array, lax.min(step + 1, count - 2), False).start()
+
+    @pl.loop(0, max(blocks, count - 1))
+    def _(step):
+        @pl.when(step < blocks)
+        def _():
+            sweep_strip(work, strip, step, block)
+
+        @pl.when(step < count - 1)
+        def _():
+            pass_on(0, step)
+
+        @pl.when(step < blocks)
+        def _():
+            sweep_rest(work, strip, step, block)
+
+        @pl.when(step < count - 1)
+        def _():
+            pass_on(1, step)
+
+    for copy in kept:
+        copy.wait()
+    for array in range(2):
+        for way in range(2):
+            piece(way, array, 0, True).wait_send()
+
+            @pl.loop(1, count - 1)
+            def _(step):
+                piece(way, array, step, False).wait_send()
+
+
+def gathered(value_shard, output_shard, prior):
+    count = lax.axis_size("dp")
+    rows, columns = value_shard.shape
     size = prior.shape[0]
-    block = 128
+    whole = jax.ShapeDtypeStruct((count * rows, columns), jnp.bfloat16)
     return pl.pallas_call(
-        prior_kernel,
-        out_shape=jax.ShapeDtypeStruct((size, size), jnp.float32),
-        in_specs=[pl.BlockSpec(memory_space=pltpu.VMEM)],
-        out_specs=pl.BlockSpec(memory_space=pltpu.VMEM),
-        scratch_shapes=[pltpu.VMEM((block, size), jnp.float32)],
-        compiler_params=pltpu.CompilerParams(vmem_limit_bytes=24 * 2**20),
-        cost_estimate=pl.CostEstimate(flops=10**11, bytes_accessed=8 * size * size, transcendentals=0),
-        name="prior_inverse",
-    )(prior)
+        functools.partial(gather_kernel, count),
+        out_shape=(whole, whole, jax.ShapeDtypeStruct((size, size), jnp.float32)),
+        in_specs=[pl.BlockSpec(memory_space=pltpu.VMEM)] * 3,
+        out_specs=(
+            pl.BlockSpec(memory_space=pl.ANY),
+            pl.BlockSpec(memory_space=pl.ANY),
+            pl.BlockSpec(memory_space=pltpu.VMEM),
+        ),
+        scratch_shapes=[
+            pltpu.VMEM((128, size), jnp.float32),
+            pltpu.SemaphoreType.DMA((2, 2, count - 1)),
+            pltpu.SemaphoreType.DMA((2, 2, count - 1)),
+            pltpu.SemaphoreType.DMA((2,)),
+        ],
+        compiler_params=pltpu.CompilerParams(
+            collective_id=2, has_side_effects=True, vmem_limit_bytes=48 * 2**20
+        ),
+        name="gather_and_invert",
+    )(value_shard, output_shard, prior)
 
 
 def score_kernel(everyone, negated, queries, out):
@@ -325,16 +436,12 @@
     output_projection,
     fisher_prior,
 ):
-    value_map, output_map = (
-        lax.all_gather(value_weight, "dp", axis=1, tiled=True),
-        lax.all_gather(output_weight, "dp", axis=1, tiled=True),
-    )
-    value_map = value_map[0]
-    output_map = output_map[0]
+    value_map, output_map, negated_inverse = gathered(
+        value_weight[0], output_weight[0], fisher_prior[0]
+    )
     gain = norm_gain.astype(jnp.float32)
     input_map = input_projection[0]
     output_map_small = output_projection[0]
-    negated_inverse = prior_inverse(fisher_prior[0])
     batches = lengths.shape[0]
     example_rows = inputs.shape[0] // batches
     width = inputs.shape[1]

time: 399 us -> 323 us (0.81)
  waiting for transfers between devices: 79 us -> 0 us
  Pallas kernels: 263 us -> 279 us
  between operations: 13.5 us -> 0.08 us
    all_gather x2 -> x0, waiting for transfers between devices: 77.6 us -> none  [the longest x1 77.6 us: per_device(): lax.all_gather(output_weight, 'dp', axis=1, tiled=True)]
    pallas_call x1, Pallas kernels: 172 us -> 188 us  [gathered(): pl.pallas_call(functools.partial(gather_kernel, count), out_shape=(whole,...]
  transfers between devices with their start and end apart: 2 -> 0, of which waited for: 1 -> 0; matrix products, arithmetic and copies ran while one was open for 0% -> 0% of each run, Pallas kernels for 43% -> 0%
where the time goes in v3:
time: 323 us
  Pallas kernels  279 us (86%)
  blocking collectives  36.8 us (11%)
  local copies, waits for them, and re-layouts  6.01 us (2%)
    pallas_call x1, Pallas kernels, gathered(): pl.pallas_call(functools.partial(gather_kernel, count), out_shape=(whole,...  188 us
    pallas_call x1, Pallas kernels, relay(): pl.pallas_call(functools.partial(relay_kernel, lax.axis_size('section'),...  87 us
    all_gather x1, blocking collectives, per_device(): everyone = lax.all_gather(flat, 'dp', axis=0, tiled=True)  30.5 us

profile of v3, /device:TPU:0, one launch (start us, length us, event | category | flops | bytes accessed | tf_op | source)
XLA Modules:
  0.0 322.5 jit_solution(9971630644567203761)
XLA Ops:
  0.0 0.0 copy-start.2
  0.0 1.2 copy-done.2
  1.2 0.0 copy-start.3
  1.2 1.2 copy-done.3
  2.5 0.0 copy-start.9
  2.5 0.0 copy-start.7
  2.5 188.4 %gather_and_invert.1 = (bf16[4096,1024]{1,0:T(8,128)(2,1)}, bf16[4096,1024]{1,0:T(8,128)(2,1)}, f32[1024,1024]{1,0:T(8,128)}) custom-call(bf16[512,1024]{1,0:T(8,128)(2,1)S(1)} %bitcast.9, bf16[512,1024]{1,0:T(8,128)(2,1)S(1)} %bitcast.10, f32[1024,1024]{1,0:T(8,128)} %bitcast.14), custom_call_target="tpu_custom_call" | custom-call | tf_op jit(solution)/shard_map/gather_and_invert/pallas_call | solution.py:175
  190.8 0.0 copy-done.9
  190.8 0.1 compare_convert_fusion
  190.9 0.0 copy-done.7
  190.9 0.0 copy-start.5
  190.9 0.2 broadcast_multiply_fusion.targets
  191.1 0.5 copy-done.8
  191.7 0.7 copy-done.1
  192.3 0.0 copy-done.4
  192.4 0.0 copy-done.5
  192.4 87.0 %relay.1 = f32[2,32,32]{2,1,0:T(8,128)S(1)} custom-call(bf16[2,96,4096]{2,1,0:T(8,128)(2,1)S(1)} %bitcast.8, bf16[2,96,4096]{2,1,0:T(8,128)(2,1)S(1)} %broadcast_multiply_fusion.targets, f32[1,4096]{1,0:T(1,128)S(1)} %convert_element_type.11.gain, bf16[4096,1024]{1,0:T(8,128)(2,1)} %get-tuple-element.8.value_map, ...), custom_call_target="tpu_custom_call" | custom-call | tf_op jit(solution)/shard_map/relay/pallas_call | solution.py:407
  279.4 0.1 reshape.34
  279.5 30.5 %all-gather = f32[8,2,1024]{2,1,0:T(2,128)S(1)} all-gather(f32[1,2,1024]{2,1,0:T(2,128)S(1)} %reshape.34), channel_id=1, replica_groups=mesh['section'=4,'dp'=8] {'dp'}, dimensions={0}, use_global_device_ids=true | all-gather | bytes 73728 | tf_op jit(solution)/shard_map/all_gather | solution.py:458
  310.1 0.0 copy-done.6
  310.1 0.0 copy-start
  310.1 2.2 copy-done
  312.3 3.9 %all_scores.1 = f32[16,16]{1,0:T(8,128)S(1)} custom-call(f32[16,1024]{1,0:T(8,128)S(1)} %reshape.35.everyone, f32[1024,1024]{1,0:T(8,128)S(1)} %copy-done, s32[1,16]{1,0:T(1,128)S(1)} %bitcast.13), custom_call_target="tpu_custom_call" | custom-call | tf_op jit(solution)/shard_map/all_scores/pallas_call | solution.py:215
  316.2 6.3 %psum.7 = f32[2,16]{1,0:T(2,128)} all-reduce(f32[2,16]{1,0:T(2,128)S(1)} %constant_dynamic-slice_fusion), channel_id=1, replica_groups=mesh['section'=4,'dp'=8] {'section'}, use_global_device_ids=true, to_apply=%region_0.0 | all-reduce | flops 32 | bytes 256 | tf_op jit(solution)/shard_map/psum | solution.py:463
  (7 shorter events, 0.1 us)
Async XLA Ops:
  0.0 1.2 copy-start.2
  1.2 1.2 copy-start.3
  2.5 188.4 %copy-start.9 = (s32[2]{0:T(128)S(1)}, s32[2]{0:T(128)}, u32[]{:S(2)}) copy-start(s32[2]{0:T(128)} %param.12) | copy-start | bytes 28
  2.5 188.5 %copy-start.7 = (bf16[192,4096]{1,0:T(8,128)(2,1)S(1)}, bf16[192,4096]{1,0:T(8,128)(2,1)}, u32[]{:S(2)}) copy-start(bf16[192,4096]{1,0:T(8,128)(2,1)} %param.11) | copy-start | bytes 4718596
  190.9 0.7 copy-start.8
  190.9 1.4 copy-start.1
  190.9 1.4 copy-start.4
  190.9 1.4 copy-start.5
  192.4 117.7 %copy-start.6 = (s32[16]{0:T(128)S(1)}, s32[16]{0:T(128)}, u32[]{:S(2)}) copy-start(s32[16]{0:T(128)} %param.13) | copy-start | bytes 196
  310.1 2.2 copy-start
